TPU v7x, 512 devices: a whole 4x8x8 slice. The times are simulated.
512 devices in a mesh: dp: 32 (over y, x), seq: 16 (over z, core).
Axes of the slice: x: 4, y: 8, z: 8, core: 2. Of those that a mesh axis runs over, the one named last changes fastest.
Arguments:
- states: bfloat16 [65536, 1280], P(('dp', 'seq')), parts along dimension 0, may hold values from -90 to 90
- token_kind: int32 [65536], P(('dp', 'seq')), parts along dimension 0, may hold values from 0 to 3
- episode: int32 [65536], P(('dp', 'seq')), parts along dimension 0, may hold values from 0 to 3, never falling along the last dimension, each value on 1 to 1536 neighbouring positions
- kind_table: bfloat16 [4, 1280], replicated, may hold values from -3 to 3
- w_qkv: bfloat16 [1280, 3072], replicated, may hold values from -0.15625 to 0.15625
- w_out: bfloat16 [1024, 1280], replicated, may hold values from -0.1875 to 0.1875
Outputs:
- attended: bfloat16 [65536, 1280], P(('dp', 'seq')), parts along dimension 0
There are 32 independent parts, one for each index of `dp`. A program takes and returns all parts, laid end to end along the dimension named above; an argument that names none is the same for every part. Nothing has to cross between parts.
All inputs are finite; a program needn't handle non-finite values.
Results may differ from a plain program's by a relative error of at most 0.0055.
The roundings to bfloat16 on the way count: a program that leaves them out, or rounds other values in their place, can miss the bound.
Values may be sent and summed in bfloat16 or wider, within the bound.
A program may use at most 128 MiB of HBM per device.

v0:
```python
import math
import jax
import jax.numpy as jnp
from jax import lax
from jax.sharding import PartitionSpec as P

HEADS = 16


def in_one_piece(arrays, axis, dim, along):
    both = jnp.concatenate(arrays, axis=along)
    result, at, gathered = (lax.all_gather(both, axis, axis=dim, tiled=True), 0, [])
    for a in arrays:
        gathered.append(lax.slice_in_dim(result, at, at + a.shape[along], axis=along))
        at += a.shape[along]
    return tuple(gathered)


def absorb(
    running, queries, query_place, query_episode, key_rows, value_rows, key_place, key_episode
):
    maxima, totals, summed = running
    temper = 1.0 / math.sqrt(queries.shape[2])
    scores = (
        jnp.einsum("qhd,khd->hqk", queries, key_rows, preferred_element_type=jnp.float32) * temper
    )
    allowed = (key_place[None, :] <= query_place[:, None]) & (
        key_episode[None, :] == query_episode[:, None]
    )
    scores = jnp.where(allowed[None], scores, -1e30)
    raised = jnp.maximum(maxima, jnp.max(scores, axis=2))
    shrink = jnp.exp(maxima - raised)
    weights = jnp.where(allowed[None], jnp.exp(scores - raised[:, :, None]), 0.0)
    totals = totals * shrink + jnp.sum(weights, axis=2)
    summed = summed * shrink.T[:, :, None] + jnp.einsum(
        "hqk,khd->qhd", weights.astype(jnp.bfloat16), value_rows, preferred_element_type=jnp.float32
    )
    return (raised, totals, summed)


def sweep_keys(
    running, queries, query_place, query_episode, key_rows, value_rows, key_place, key_episode
):
    length = key_rows.shape[0]
    stride = math.gcd(length, 512)

    def visit(number, current):
        offset = number * stride
        keys_here = lax.dynamic_slice_in_dim(key_rows, offset, stride, 0)
        values_here = lax.dynamic_slice_in_dim(value_rows, offset, stride, 0)
        place_here = lax.dynamic_slice_in_dim(key_place, offset, stride, 0)
        episode_here = lax.dynamic_slice_in_dim(key_episode, offset, stride, 0)
        skipped = (place_here[0] > query_place[-1]) | (episode_here[-1] < query_episode[0])
        return lax.cond(
            skipped,
            lambda s: s,
            lambda s: absorb(
                s,
                queries,
                query_place,
                query_episode,
                keys_here,
                values_here,
                place_here,
                episode_here,
            ),
            current,
        )

    return lax.fori_loop(0, length // stride, visit, running)


def fresh_state(count, heads, head_size):
    return (
        jnp.full((heads, count), -1e30, jnp.float32),
        jnp.zeros((heads, count), jnp.float32),
        jnp.zeros((count, heads, head_size), jnp.float32),
    )


def local(states, token_kind, episode, kind_table, w_qkv, w_out):
    rows = states.shape[0]
    kinds = kind_table.shape[0]
    picked = (token_kind[:, None] == jnp.arange(kinds, dtype=jnp.int32)[None, :]).astype(
        jnp.float32
    )
    added = jnp.dot(picked, kind_table.astype(jnp.float32))
    inputs = (states.astype(jnp.float32) + added).astype(jnp.bfloat16)
    projected = jnp.dot(inputs, w_qkv, preferred_element_type=jnp.float32).astype(jnp.bfloat16)
    inner = w_out.shape[0]
    head_size = inner // HEADS
    queries = projected[:, :inner].reshape(rows, HEADS, head_size)
    key_flat = projected[:, inner : 2 * inner]
    value_flat = projected[:, 2 * inner :]
    own_place = lax.axis_index("seq") * rows + jnp.arange(rows, dtype=jnp.int32)
    key_piece, value_piece, episode_piece = (
        *in_one_piece((key_flat, value_flat), "seq", 0, 1),
        lax.all_gather(episode, "seq", axis=0, tiled=True),
    )
    count = key_piece.shape[0]
    piece_place = jnp.arange(count, dtype=jnp.int32)
    maxima, totals, summed = sweep_keys(
        fresh_state(rows, HEADS, head_size),
        queries,
        own_place,
        episode,
        key_piece.reshape(count, HEADS, head_size),
        value_piece.reshape(count, HEADS, head_size),
        piece_place,
        episode_piece,
    )
    heads_out = (summed / totals.T[:, :, None]).astype(jnp.bfloat16).reshape(rows, inner)
    return jnp.dot(heads_out, w_out, preferred_element_type=jnp.float32).astype(jnp.bfloat16)


def solution(mesh):
    placed = (P(("dp", "seq"), None), P(("dp", "seq")), P(("dp", "seq")), P(), P(), P())
    return jax.shard_map(
        local, mesh=mesh, in_specs=placed, out_specs=P(("dp", "seq"), None), check_vma=False
    )
```

profile of v0, /device:TPU:387, one launch (start us, length us, event | category | flops | bytes accessed | tf_op | source)
XLA Modules:
  0.0 137.9 jit_solution(9066481034130938527)
XLA Ops:
  6.5 0.0 copy-start
  6.5 0.0 copy-start.1
  6.5 0.0 all-gather.3.cloned.1.call-start
  6.5 4.9 %convolution_convert_fusion = bf16[128,3072]{1,0:T(8,128)(2,1)S(1)} fusion(bf16[1280,3072]{1,0:T(8,128)(2,1)} %param.14, bf16[4,1280]{1,0:T(4,128)(2,1)} %param.13, bf16[128,1280]{1,0:T(8,128)(2,1)} %param.10, s32[128]{0:T(128)} %param.11), kind=kOutput, calls=%fused_computation.21 | convolution fusion | flops 1008828928 | bytes 8989184 | tf_op jit(solution)/shard_map/dot_general | solution.py:89
  11.4 0.9 concatenate.4
  12.3 0.0 all-gather.3.cloned.1.call-update
  12.3 0.7 slice.44
  13.1 1.1 copy.17
  14.2 0.0 copy-done.1
  14.2 14.9 %all-gather = s32[16,1,128]{2,1,0:T(1,128)S(1)} all-gather(s32[1,1,128]{2,1,0:T(1,128)S(1)} %bitcast.45), channel_id=1, replica_groups=mesh['dp'=32,'seq'=16] {'seq'}, dimensions={0}, use_global_device_ids=true | all-gather | bytes 8704 | tf_op jit(solution)/shard_map/all_gather | solution.py:98
  29.1 40.7 %all-gather.3.cloned.1.call-done = bf16[2048,2048]{1,0:T(8,128)(2,1)} async-done(((bf16[128,2048]{1,0:T(8,128)(2,1)}), bf16[2048,2048]{1,0:T(8,128)(2,1)}) %all-gather.3.cloned.1.call-update) | async-done | bytes 8388624 | tf_op jit(solution)/shard_map/all_gather | solution.py:12
  69.8 5.9 %fusion.25 = (bf16[2048,1024]{1,0:T(8,128)(2,1)}, bf16[2048,1024]{1,0:T(8,128)(2,1)}) fusion(bf16[2048,2048]{1,0:T(8,128)(2,1)} %all-gather.3.cloned.1.call-done), kind=kLoop, calls=%fused_computation.30 | loop fusion | bytes 16777216 | tf_op jit(solution)/shard_map/slice | solution.py:14
  75.7 6.5 %copy.16 = bf16[2048,1024]{0,1:T(8,128)(2,1)} copy(bf16[2048,1024]{1,0:T(8,128)(2,1)} %get-tuple-element.331) | data formatting | bytes 8388608 | tf_op jit(solution)/shard_map/slice | solution.py:14
  82.2 6.5 %copy.18 = bf16[2048,1024]{0,1:T(8,128)(2,1)} copy(bf16[2048,1024]{1,0:T(8,128)(2,1)} %get-tuple-element.330) | data formatting | bytes 8388608 | tf_op jit(solution)/shard_map/slice | solution.py:14
  88.8 40.9 %while.17 = (s32[]{:T(128)}, f32[16,128]{1,0:T(8,128)S(1)}, f32[16,128]{1,0:T(8,128)S(1)}, f32[128,16,64]{0,2,1:T(8,128)S(1)}, s32[2048]{0:T(1024)S(1)}, /*index...) while((s32[]{:T(128)}, f32[16,128]{1,0:T(8,128)S(1)}, ...), condition=%wide.region_5.6_spmd, body=%wide.region_0.5_spmd.sunk | while | flops 282531840 | bytes 16398717 | solution.py:70
  88.8 0.1 dynamic_slice.46
  88.9 0.1 dynamic_slice.47
  89.0 0.6 slice.51
  89.5 0.6 slice.52
  91.5 0.6 slice.53
  92.8 6.2 %conditional.2 = (f32[16,128]{1,0:T(8,128)S(1)}, f32[16,128]{1,0:T(8,128)S(1)}, f32[128,16,64]{0,2,1:T(8,128)S(1)}) conditional(s32[]{:T(128)} %bitcast.38, (s32[512]{0:T(512)S(1)}, s32[128]{0:T(128)S(1)}, s32[512]{0:T(512)S(1)}, s32[128]{0:T(128)S(1)}, bf16[2048,16,64]{0,2,1:T(8,128)(2,1)}, /*index=5*/s32[]{:T(128)}, ...), branch_computations={%region_1.3_spmd, %region_4.4_spmd} | conditional | flops 282531840 | bytes 16373784 | solution.py:54
  92.8 0.2 compare_and_fusion
  93.0 2.2 %fusion = (f32[16,128]{1,0:T(8,128)S(1)}, f32[16,512,128]{2,1,0:T(8,128)S(1)}) fusion(pred[128,512]{0,1:T(8,128)(4,1)S(1)} %compare_and_fusion, bf16[128,16,64]{0,2,1:T(8,128)(2,1)S(1)} %get-tuple-element.270, bf16[2048,16,64]{0,2,1:T(8,128)(2,1)} %get-tuple-element.268, s32[]{:T(128)} %get-tuple-element.269), kind=kOutput, calls=%fused_computation.2 | convolution fusion | flops 137361408 | bytes 5579264 | tf_op jit(solution)/shard_map/while/body/eval_jaxpr/cond/branch_0_fun/qhd,khd->hqk/dot_general | solution.py:25
  95.3 2.7 %fusion.9 = f32[128,16,64]{0,2,1:T(8,128)S(1)} fusion(f32[16,512,128]{2,1,0:T(8,128)S(1)} %get-tuple-element.329, f32[16,128]{1,0:T(8,128)S(1)} %get-tuple-element.405, pred[128,512]{0,1:T(8,128)(4,1)S(1)} %compare_and_fusion, bf16[2048,16,64]{0,2,1:T(8,128)(2,1)} %get-tuple-element.273, s32[]{:T(128)} %get-tuple-element.269, ...), kind=kOutput, calls=%fused_computation.8 | convolution fusion | flops 139722752 | bytes 6373888 | tf_op jit(solution)/shard_map/while/body/eval_jaxpr/cond/branch_0_fun/hqk,khd->qhd/dot_general | solution.py:35
  98.0 1.0 fusion.2
  99.0 0.1 dynamic_slice.46
  99.1 0.1 dynamic_slice.47
  99.2 0.6 slice.51
  99.8 0.6 slice.52
  101.7 0.6 slice.53
  103.0 6.2 %conditional.2 = (f32[16,128]{1,0:T(8,128)S(1)}, f32[16,128]{1,0:T(8,128)S(1)}, f32[128,16,64]{0,2,1:T(8,128)S(1)}) conditional(s32[]{:T(128)} %bitcast.38, (s32[512]{0:T(512)S(1)}, s32[128]{0:T(128)S(1)}, s32[512]{0:T(512)S(1)}, s32[128]{0:T(128)S(1)}, bf16[2048,16,64]{0,2,1:T(8,128)(2,1)}, /*index=5*/s32[]{:T(128)}, ...), branch_computations={%region_1.3_spmd, %region_4.4_spmd} | conditional | flops 282531840 | bytes 16373784 | solution.py:54
  103.0 0.2 compare_and_fusion
  103.2 2.2 %fusion = (f32[16,128]{1,0:T(8,128)S(1)}, f32[16,512,128]{2,1,0:T(8,128)S(1)}) fusion(pred[128,512]{0,1:T(8,128)(4,1)S(1)} %compare_and_fusion, bf16[128,16,64]{0,2,1:T(8,128)(2,1)S(1)} %get-tuple-element.270, bf16[2048,16,64]{0,2,1:T(8,128)(2,1)} %get-tuple-element.268, s32[]{:T(128)} %get-tuple-element.269), kind=kOutput, calls=%fused_computation.2 | convolution fusion | flops 137361408 | bytes 5579264 | tf_op jit(solution)/shard_map/while/body/eval_jaxpr/cond/branch_0_fun/qhd,khd->hqk/dot_general | solution.py:25
  105.5 2.7 %fusion.9 = f32[128,16,64]{0,2,1:T(8,128)S(1)} fusion(f32[16,512,128]{2,1,0:T(8,128)S(1)} %get-tuple-element.329, f32[16,128]{1,0:T(8,128)S(1)} %get-tuple-element.405, pred[128,512]{0,1:T(8,128)(4,1)S(1)} %compare_and_fusion, bf16[2048,16,64]{0,2,1:T(8,128)(2,1)} %get-tuple-element.273, s32[]{:T(128)} %get-tuple-element.269, ...), kind=kOutput, calls=%fused_computation.8 | convolution fusion | flops 139722752 | bytes 6373888 | tf_op jit(solution)/shard_map/while/body/eval_jaxpr/cond/branch_0_fun/hqk,khd->qhd/dot_general | solution.py:35
  108.2 1.0 fusion.2
  109.2 0.1 dynamic_slice.46
  109.3 0.1 dynamic_slice.47
  109.4 0.6 slice.51
  110.0 0.6 slice.52
  111.9 0.6 slice.53
  113.2 6.2 %conditional.2 = (f32[16,128]{1,0:T(8,128)S(1)}, f32[16,128]{1,0:T(8,128)S(1)}, f32[128,16,64]{0,2,1:T(8,128)S(1)}) conditional(s32[]{:T(128)} %bitcast.38, (s32[512]{0:T(512)S(1)}, s32[128]{0:T(128)S(1)}, s32[512]{0:T(512)S(1)}, s32[128]{0:T(128)S(1)}, bf16[2048,16,64]{0,2,1:T(8,128)(2,1)}, /*index=5*/s32[]{:T(128)}, ...), branch_computations={%region_1.3_spmd, %region_4.4_spmd} | conditional | flops 282531840 | bytes 16373784 | solution.py:54
  113.2 0.2 compare_and_fusion
  113.4 2.2 %fusion = (f32[16,128]{1,0:T(8,128)S(1)}, f32[16,512,128]{2,1,0:T(8,128)S(1)}) fusion(pred[128,512]{0,1:T(8,128)(4,1)S(1)} %compare_and_fusion, bf16[128,16,64]{0,2,1:T(8,128)(2,1)S(1)} %get-tuple-element.270, bf16[2048,16,64]{0,2,1:T(8,128)(2,1)} %get-tuple-element.268, s32[]{:T(128)} %get-tuple-element.269), kind=kOutput, calls=%fused_computation.2 | convolution fusion | flops 137361408 | bytes 5579264 | tf_op jit(solution)/shard_map/while/body/eval_jaxpr/cond/branch_0_fun/qhd,khd->hqk/dot_general | solution.py:25
  115.7 2.7 %fusion.9 = f32[128,16,64]{0,2,1:T(8,128)S(1)} fusion(f32[16,512,128]{2,1,0:T(8,128)S(1)} %get-tuple-element.329, f32[16,128]{1,0:T(8,128)S(1)} %get-tuple-element.405, pred[128,512]{0,1:T(8,128)(4,1)S(1)} %compare_and_fusion, bf16[2048,16,64]{0,2,1:T(8,128)(2,1)} %get-tuple-element.273, s32[]{:T(128)} %get-tuple-element.269, ...), kind=kOutput, calls=%fused_computation.8 | convolution fusion | flops 139722752 | bytes 6373888 | tf_op jit(solution)/shard_map/while/body/eval_jaxpr/cond/branch_0_fun/hqk,khd->qhd/dot_general | solution.py:35
  118.4 1.0 fusion.2
  119.5 0.1 dynamic_slice.46
  119.5 0.1 dynamic_slice.47
  119.6 0.6 slice.51
  120.2 0.6 slice.52
  122.1 0.6 slice.53
  123.4 6.2 %conditional.2 = (f32[16,128]{1,0:T(8,128)S(1)}, f32[16,128]{1,0:T(8,128)S(1)}, f32[128,16,64]{0,2,1:T(8,128)S(1)}) conditional(s32[]{:T(128)} %bitcast.38, (s32[512]{0:T(512)S(1)}, s32[128]{0:T(128)S(1)}, s32[512]{0:T(512)S(1)}, s32[128]{0:T(128)S(1)}, bf16[2048,16,64]{0,2,1:T(8,128)(2,1)}, /*index=5*/s32[]{:T(128)}, ...), branch_computations={%region_1.3_spmd, %region_4.4_spmd} | conditional | flops 282531840 | bytes 16373784 | solution.py:54
  123.5 0.2 compare_and_fusion
  123.7 2.2 %fusion = (f32[16,128]{1,0:T(8,128)S(1)}, f32[16,512,128]{2,1,0:T(8,128)S(1)}) fusion(pred[128,512]{0,1:T(8,128)(4,1)S(1)} %compare_and_fusion, bf16[128,16,64]{0,2,1:T(8,128)(2,1)S(1)} %get-tuple-element.270, bf16[2048,16,64]{0,2,1:T(8,128)(2,1)} %get-tuple-element.268, s32[]{:T(128)} %get-tuple-element.269), kind=kOutput, calls=%fused_computation.2 | convolution fusion | flops 137361408 | bytes 5579264 | tf_op jit(solution)/shard_map/while/body/eval_jaxpr/cond/branch_0_fun/qhd,khd->hqk/dot_general | solution.py:25
  125.9 2.7 %fusion.9 = f32[128,16,64]{0,2,1:T(8,128)S(1)} fusion(f32[16,512,128]{2,1,0:T(8,128)S(1)} %get-tuple-element.329, f32[16,128]{1,0:T(8,128)S(1)} %get-tuple-element.405, pred[128,512]{0,1:T(8,128)(4,1)S(1)} %compare_and_fusion, bf16[2048,16,64]{0,2,1:T(8,128)(2,1)} %get-tuple-element.273, s32[]{:T(128)} %get-tuple-element.269, ...), kind=kOutput, calls=%fused_computation.8 | convolution fusion | flops 139722752 | bytes 6373888 | tf_op jit(solution)/shard_map/while/body/eval_jaxpr/cond/branch_0_fun/hqk,khd->qhd/dot_general | solution.py:35
  128.6 1.0 fusion.2
  129.7 0.1 divide_convert_fusion
  129.7 0.0 copy-done
  129.7 1.3 convolution_convert_fusion.1
  (17 shorter events, 0.1 us)
Async XLA Ops:
  6.5 123.2 %copy-start = (bf16[1024,1280]{1,0:T(8,128)(2,1)S(1)}, bf16[1024,1280]{1,0:T(8,128)(2,1)}, u32[]{:S(2)}) copy-start(bf16[1024,1280]{1,0:T(8,128)(2,1)} %param.15) | copy-start | bytes 7864324
  6.5 7.6 %copy-start.1 = (s32[128]{0:T(128)S(1)}, s32[128]{0:T(128)}, u32[]{:S(2)}) copy-start(s32[128]{0:T(128)} %param.12) | copy-start | bytes 1540
  6.5 63.2 %all-gather.3.cloned.1.call-start = ((), (), s32[]{:S(2)}) async-start(), calls=%async_computation | async-start | bytes 8912896 | tf_op jit(solution)/shard_map/all_gather | solution.py:12
Sparse Core Ops, SparseCore 0:
  12.5 57.2 all-gather.2
where the time goes:
time: 139 us; the launch traced here: 138 us
  waiting for transfers between devices  40.7 us (29%)
  local copies, waits for them, and re-layouts  29.7 us (21%)
  matrix products  25.8 us (19%)
  blocking collectives  14.9 us (11%)
  between operations  13.5 us (10%)
  loops' own time  8.33 us (6%)
  other arithmetic  4.96 us (4%)
    all_gather x1, waiting for transfers between devices, in_one_piece(): lax.all_gather(both, axis, axis=dim, tiled=True)  40.7 us
    slice x3, local copies, waits for them, and re-layouts, in_one_piece(): lax.slice_in_dim(result, at, at + a.shape[along], axis=along)  18.9 us
    all_gather x1, blocking collectives, local(): lax.all_gather(episode, 'seq', axis=0, tiled=True)  14.9 us
    dot_general x4, matrix products, absorb(): jnp.einsum('hqk,khd->qhd', weights.astype(jnp.bfloat16), value_rows, pref...  10.7 us
    dot_general x4, matrix products, absorb(): jnp.einsum('qhd,khd->hqk', queries, key_rows, preferred_element_type=jnp....  8.94 us
    another operation x1, loops' own time, sweep_keys(): return lax.fori_loop(0, length // stride, visit, running)  8.14 us
    dot_general x1, matrix products, local(): jnp.dot(inputs, w_qkv, preferred_element_type=jnp.float32)  4.89 us
    reduce_sum x4, other arithmetic, absorb(): totals = totals * shrink + jnp.sum(weights, axis=2)  4.01 us
  transfers between devices with their start and end apart: 1, of which 1 were waited for; matrix products, arithmetic and copies ran while one was open for 1% of the time, Pallas kernels for 0%

commit v1 on v0

--- a/solution.py
+++ b/solution.py
@@ -95,7 +95,9 @@
     own_place = lax.axis_index("seq") * rows + jnp.arange(rows, dtype=jnp.int32)
     key_piece, value_piece, episode_piece = (
         *in_one_piece((key_flat, value_flat), "seq", 0, 1),
-        lax.all_gather(episode, "seq", axis=0, tiled=True),
+        jnp.concatenate(
+            lax.all_to_all(jnp.stack([episode] * lax.axis_size("seq")), "seq", 0, 0), axis=0
+        ),
     )
     count = key_piece.shape[0]
     piece_place = jnp.arange(count, dtype=jnp.int32)

time: 139 us -> 140 us (level)
  blocking collectives: 14.9 us -> 0 us
  waiting for transfers between devices: 40.7 us -> 50 us
  starting transfers between devices: 0.01 us -> 5.72 us
    all_gather x1 -> x0, blocking collectives: 14.9 us -> none  [local(): lax.all_gather(episode, 'seq', axis=0, tiled=True)]
    all_gather x1, waiting for transfers between devices: 40.7 us -> 49.9 us  [in_one_piece(): lax.all_gather(both, axis, axis=dim, tiled=True)]
    all_to_all x0 -> x1, starting transfers between devices: none -> 5.72 us  [local(): lax.all_to_all(jnp.stack([episode] * lax.axis_size('seq')), 'seq', 0, 0)]
  transfers between devices with their start and end apart: 1 -> 2, of which waited for: 1 -> 1; matrix products, arithmetic and copies ran while one was open for 1% -> 15% of each run, Pallas kernels for 0% -> 0%
where the time goes in v1:
time: 140 us
  waiting for transfers between devices  50 us (36%)
  local copies, waits for them, and re-layouts  30.5 us (22%)
  matrix products  26.8 us (19%)
  between operations  13.5 us (10%)
  loops' own time  8.19 us (6%)
  starting transfers between devices  5.72 us (4%)
  other arithmetic  4.96 us (4%)
    all_gather x1, waiting for transfers between devices, in_one_piece(): lax.all_gather(both, axis, axis=dim, tiled=True)  49.9 us
    slice x3, local copies, waits for them, and re-layouts, in_one_piece(): lax.slice_in_dim(result, at, at + a.shape[along], axis=along)  18.9 us
    dot_general x4, matrix products, absorb(): jnp.einsum('hqk,khd->qhd', weights.astype(jnp.bfloat16), value_rows, pref...  10.7 us
    dot_general x4, matrix products, absorb(): jnp.einsum('qhd,khd->hqk', queries, key_rows, preferred_element_type=jnp....  8.94 us
    another operation x1, loops' own time, sweep_keys(): return lax.fori_loop(0, length // stride, visit, running)  8 us
    dot_general x1, matrix products, local(): jnp.dot(inputs, w_qkv, preferred_element_type=jnp.float32)  5.84 us
    all_to_all x1, starting transfers between devices, local(): lax.all_to_all(jnp.stack([episode] * lax.axis_size('seq')), 'seq', 0, 0)  5.72 us
    reduce_sum x4, other arithmetic, absorb(): totals = totals * shrink + jnp.sum(weights, axis=2)  4.01 us
  transfers between devices with their start and end apart: 2, of which 1 were waited for; matrix products, arithmetic and copies ran while one was open for 15% of the time, Pallas kernels for 0%

profile of v1, /device:TPU:387, one launch (start us, length us, event | category | flops | bytes accessed | tf_op | source)
XLA Modules:
  0.0 139.6 jit_solution(15195682838775643419)
XLA Ops:
  6.5 0.0 copy-start
  6.5 0.0 copy-start.1
  6.5 0.0 all-gather.2.cloned.1.call-start
  6.5 5.8 %convolution_convert_fusion = bf16[128,3072]{1,0:T(8,128)(2,1)} fusion(bf16[1280,3072]{1,0:T(8,128)(2,1)} %param.14, bf16[4,1280]{1,0:T(4,128)(2,1)} %param.13, bf16[128,1280]{1,0:T(8,128)(2,1)} %param.10, s32[128]{0:T(128)} %param.11), kind=kOutput, calls=%fused_computation.21 | convolution fusion | flops 1008828928 | bytes 8989184 | tf_op jit(solution)/shard_map/dot_general | solution.py:89
  12.4 1.9 %concatenate.4 = bf16[128,2048]{1,0:T(8,128)(2,1)} slice(bf16[128,3072]{1,0:T(8,128)(2,1)} %convolution_convert_fusion), slice={[0:128], [1024:3072]} | slice | bytes 1048576 | tf_op jit(solution)/shard_map/concatenate | solution.py:11
  14.3 0.0 all-gather.2.cloned.1.call-update
  14.3 0.0 copy-done.1
  14.3 0.6 stack.2
  14.9 5.7 %all-to-all-start = ((s32[16,1,128]{2,1,0:T(1,128)}), s32[16,1,128]{2,1,0:T(1,128)S(1)}, u32[]{:S(2)}, u32[]{:S(2)}) async-start(s32[16,1,128]{2,1,0:T(1,128)} %stack.2), calls=%async_computation | async-start | bytes 16384 | tf_op jit(solution)/shard_map/all_to_all | solution.py:99
  20.6 1.0 slice.44
  21.6 0.2 copy.13
  21.8 49.9 %all-gather.2.cloned.1.call-done = bf16[2048,2048]{1,0:T(8,128)(2,1)} async-done(((bf16[128,2048]{1,0:T(8,128)(2,1)}), bf16[2048,2048]{1,0:T(8,128)(2,1)}) %all-gather.2.cloned.1.call-update) | async-done | bytes 8388624 | tf_op jit(solution)/shard_map/all_gather | solution.py:12
  71.7 5.9 %fusion.25 = (bf16[2048,1024]{1,0:T(8,128)(2,1)}, bf16[2048,1024]{1,0:T(8,128)(2,1)}) fusion(bf16[2048,2048]{1,0:T(8,128)(2,1)} %all-gather.2.cloned.1.call-done), kind=kLoop, calls=%fused_computation.30 | loop fusion | bytes 16777216 | tf_op jit(solution)/shard_map/slice | solution.py:14
  77.6 6.5 %copy.12 = bf16[2048,1024]{0,1:T(8,128)(2,1)} copy(bf16[2048,1024]{1,0:T(8,128)(2,1)} %get-tuple-element.331) | data formatting | bytes 8388608 | tf_op jit(solution)/shard_map/slice | solution.py:14
  84.2 6.5 %copy.14 = bf16[2048,1024]{0,1:T(8,128)(2,1)} copy(bf16[2048,1024]{1,0:T(8,128)(2,1)} %get-tuple-element.330) | data formatting | bytes 8388608 | tf_op jit(solution)/shard_map/slice | solution.py:14
  90.7 0.0 all-to-all-done
  90.7 40.6 %while.17 = (s32[]{:T(128)}, f32[16,128]{1,0:T(8,128)S(1)}, f32[16,128]{1,0:T(8,128)S(1)}, f32[128,16,64]{0,2,1:T(8,128)S(1)}, s32[2048]{0:T(1024)S(1)}, /*index...) while((s32[]{:T(128)}, f32[16,128]{1,0:T(8,128)S(1)}, ...), condition=%wide.region_5.6_spmd, body=%wide.region_0.5_spmd.sunk | while | flops 282531840 | bytes 16398717 | solution.py:70
  90.8 0.1 dynamic_slice.46
  90.8 0.1 dynamic_slice.47
  90.9 0.5 slice.51
  91.5 0.6 slice.52
  93.4 0.6 slice.53
  94.7 6.2 %conditional.2 = (f32[16,128]{1,0:T(8,128)S(1)}, f32[16,128]{1,0:T(8,128)S(1)}, f32[128,16,64]{0,2,1:T(8,128)S(1)}) conditional(s32[]{:T(128)} %bitcast.37, (s32[512]{0:T(512)S(1)}, s32[128]{0:T(128)S(1)}, s32[512]{0:T(512)S(1)}, s32[128]{0:T(128)S(1)}, bf16[2048,16,64]{0,2,1:T(8,128)(2,1)}, /*index=5*/s32[]{:T(128)}, ...), branch_computations={%region_1.3_spmd, %region_4.4_spmd} | conditional | flops 282531840 | bytes 16373784 | solution.py:54
  94.7 0.2 compare_and_fusion
  94.9 2.2 %fusion = (f32[16,128]{1,0:T(8,128)S(1)}, f32[16,512,128]{2,1,0:T(8,128)S(1)}) fusion(pred[128,512]{0,1:T(8,128)(4,1)S(1)} %compare_and_fusion, bf16[128,16,64]{0,2,1:T(8,128)(2,1)S(1)} %get-tuple-element.270, bf16[2048,16,64]{0,2,1:T(8,128)(2,1)} %get-tuple-element.268, s32[]{:T(128)} %get-tuple-element.269), kind=kOutput, calls=%fused_computation.2 | convolution fusion | flops 137361408 | bytes 5579264 | tf_op jit(solution)/shard_map/while/body/eval_jaxpr/cond/branch_0_fun/qhd,khd->hqk/dot_general | solution.py:25
  97.2 2.7 %fusion.9 = f32[128,16,64]{0,2,1:T(8,128)S(1)} fusion(f32[16,512,128]{2,1,0:T(8,128)S(1)} %get-tuple-element.329, f32[16,128]{1,0:T(8,128)S(1)} %get-tuple-element.405, pred[128,512]{0,1:T(8,128)(4,1)S(1)} %compare_and_fusion, bf16[2048,16,64]{0,2,1:T(8,128)(2,1)} %get-tuple-element.273, s32[]{:T(128)} %get-tuple-element.269, ...), kind=kOutput, calls=%fused_computation.8 | convolution fusion | flops 139722752 | bytes 6373888 | tf_op jit(solution)/shard_map/while/body/eval_jaxpr/cond/branch_0_fun/hqk,khd->qhd/dot_general | solution.py:35
  99.8 1.0 fusion.2
  100.9 0.1 dynamic_slice.46
  101.0 0.1 dynamic_slice.47
  101.1 0.5 slice.51
  101.6 0.6 slice.52
  103.6 0.6 slice.53
  104.8 6.2 %conditional.2 = (f32[16,128]{1,0:T(8,128)S(1)}, f32[16,128]{1,0:T(8,128)S(1)}, f32[128,16,64]{0,2,1:T(8,128)S(1)}) conditional(s32[]{:T(128)} %bitcast.37, (s32[512]{0:T(512)S(1)}, s32[128]{0:T(128)S(1)}, s32[512]{0:T(512)S(1)}, s32[128]{0:T(128)S(1)}, bf16[2048,16,64]{0,2,1:T(8,128)(2,1)}, /*index=5*/s32[]{:T(128)}, ...), branch_computations={%region_1.3_spmd, %region_4.4_spmd} | conditional | flops 282531840 | bytes 16373784 | solution.py:54
  104.8 0.2 compare_and_fusion
  105.1 2.2 %fusion = (f32[16,128]{1,0:T(8,128)S(1)}, f32[16,512,128]{2,1,0:T(8,128)S(1)}) fusion(pred[128,512]{0,1:T(8,128)(4,1)S(1)} %compare_and_fusion, bf16[128,16,64]{0,2,1:T(8,128)(2,1)S(1)} %get-tuple-element.270, bf16[2048,16,64]{0,2,1:T(8,128)(2,1)} %get-tuple-element.268, s32[]{:T(128)} %get-tuple-element.269), kind=kOutput, calls=%fused_computation.2 | convolution fusion | flops 137361408 | bytes 5579264 | tf_op jit(solution)/shard_map/while/body/eval_jaxpr/cond/branch_0_fun/qhd,khd->hqk/dot_general | solution.py:25
  107.3 2.7 %fusion.9 = f32[128,16,64]{0,2,1:T(8,128)S(1)} fusion(f32[16,512,128]{2,1,0:T(8,128)S(1)} %get-tuple-element.329, f32[16,128]{1,0:T(8,128)S(1)} %get-tuple-element.405, pred[128,512]{0,1:T(8,128)(4,1)S(1)} %compare_and_fusion, bf16[2048,16,64]{0,2,1:T(8,128)(2,1)} %get-tuple-element.273, s32[]{:T(128)} %get-tuple-element.269, ...), kind=kOutput, calls=%fused_computation.8 | convolution fusion | flops 139722752 | bytes 6373888 | tf_op jit(solution)/shard_map/while/body/eval_jaxpr/cond/branch_0_fun/hqk,khd->qhd/dot_general | solution.py:35
  110.0 1.0 fusion.2
  111.1 0.1 dynamic_slice.46
  111.1 0.1 dynamic_slice.47
  111.2 0.5 slice.51
  111.8 0.6 slice.52
  113.7 0.6 slice.53
  115.0 6.2 %conditional.2 = (f32[16,128]{1,0:T(8,128)S(1)}, f32[16,128]{1,0:T(8,128)S(1)}, f32[128,16,64]{0,2,1:T(8,128)S(1)}) conditional(s32[]{:T(128)} %bitcast.37, (s32[512]{0:T(512)S(1)}, s32[128]{0:T(128)S(1)}, s32[512]{0:T(512)S(1)}, s32[128]{0:T(128)S(1)}, bf16[2048,16,64]{0,2,1:T(8,128)(2,1)}, /*index=5*/s32[]{:T(128)}, ...), branch_computations={%region_1.3_spmd, %region_4.4_spmd} | conditional | flops 282531840 | bytes 16373784 | solution.py:54
  115.0 0.2 compare_and_fusion
  115.2 2.2 %fusion = (f32[16,128]{1,0:T(8,128)S(1)}, f32[16,512,128]{2,1,0:T(8,128)S(1)}) fusion(pred[128,512]{0,1:T(8,128)(4,1)S(1)} %compare_and_fusion, bf16[128,16,64]{0,2,1:T(8,128)(2,1)S(1)} %get-tuple-element.270, bf16[2048,16,64]{0,2,1:T(8,128)(2,1)} %get-tuple-element.268, s32[]{:T(128)} %get-tuple-element.269), kind=kOutput, calls=%fused_computation.2 | convolution fusion | flops 137361408 | bytes 5579264 | tf_op jit(solution)/shard_map/while/body/eval_jaxpr/cond/branch_0_fun/qhd,khd->hqk/dot_general | solution.py:25
  117.5 2.7 %fusion.9 = f32[128,16,64]{0,2,1:T(8,128)S(1)} fusion(f32[16,512,128]{2,1,0:T(8,128)S(1)} %get-tuple-element.329, f32[16,128]{1,0:T(8,128)S(1)} %get-tuple-element.405, pred[128,512]{0,1:T(8,128)(4,1)S(1)} %compare_and_fusion, bf16[2048,16,64]{0,2,1:T(8,128)(2,1)} %get-tuple-element.273, s32[]{:T(128)} %get-tuple-element.269, ...), kind=kOutput, calls=%fused_computation.8 | convolution fusion | flops 139722752 | bytes 6373888 | tf_op jit(solution)/shard_map/while/body/eval_jaxpr/cond/branch_0_fun/hqk,khd->qhd/dot_general | solution.py:35
  120.2 1.0 fusion.2
  121.2 0.1 dynamic_slice.46
  121.3 0.1 dynamic_slice.47
  121.4 0.5 slice.51
  121.9 0.6 slice.52
  123.9 0.6 slice.53
  125.2 6.2 %conditional.2 = (f32[16,128]{1,0:T(8,128)S(1)}, f32[16,128]{1,0:T(8,128)S(1)}, f32[128,16,64]{0,2,1:T(8,128)S(1)}) conditional(s32[]{:T(128)} %bitcast.37, (s32[512]{0:T(512)S(1)}, s32[128]{0:T(128)S(1)}, s32[512]{0:T(512)S(1)}, s32[128]{0:T(128)S(1)}, bf16[2048,16,64]{0,2,1:T(8,128)(2,1)}, /*index=5*/s32[]{:T(128)}, ...), branch_computations={%region_1.3_spmd, %region_4.4_spmd} | conditional | flops 282531840 | bytes 16373784 | solution.py:54
  125.2 0.2 compare_and_fusion
  125.4 2.2 %fusion = (f32[16,128]{1,0:T(8,128)S(1)}, f32[16,512,128]{2,1,0:T(8,128)S(1)}) fusion(pred[128,512]{0,1:T(8,128)(4,1)S(1)} %compare_and_fusion, bf16[128,16,64]{0,2,1:T(8,128)(2,1)S(1)} %get-tuple-element.270, bf16[2048,16,64]{0,2,1:T(8,128)(2,1)} %get-tuple-element.268, s32[]{:T(128)} %get-tuple-element.269), kind=kOutput, calls=%fused_computation.2 | convolution fusion | flops 137361408 | bytes 5579264 | tf_op jit(solution)/shard_map/while/body/eval_jaxpr/cond/branch_0_fun/qhd,khd->hqk/dot_general | solution.py:25
  127.6 2.7 %fusion.9 = f32[128,16,64]{0,2,1:T(8,128)S(1)} fusion(f32[16,512,128]{2,1,0:T(8,128)S(1)} %get-tuple-element.329, f32[16,128]{1,0:T(8,128)S(1)} %get-tuple-element.405, pred[128,512]{0,1:T(8,128)(4,1)S(1)} %compare_and_fusion, bf16[2048,16,64]{0,2,1:T(8,128)(2,1)} %get-tuple-element.273, s32[]{:T(128)} %get-tuple-element.269, ...), kind=kOutput, calls=%fused_computation.8 | convolution fusion | flops 139722752 | bytes 6373888 | tf_op jit(solution)/shard_map/while/body/eval_jaxpr/cond/branch_0_fun/hqk,khd->qhd/dot_general | solution.py:35
  130.3 1.0 fusion.2
  131.4 0.1 divide_convert_fusion
  131.4 0.0 copy-done
  131.5 1.3 convolution_convert_fusion.1
  (17 shorter events, 0.1 us)
Async XLA Ops:
  6.5 124.9 %copy-start = (bf16[1024,1280]{1,0:T(8,128)(2,1)S(1)}, bf16[1024,1280]{1,0:T(8,128)(2,1)}, u32[]{:S(2)}) copy-start(bf16[1024,1280]{1,0:T(8,128)(2,1)} %param.15) | copy-start | bytes 7864324
  6.5 7.8 %copy-start.1 = (s32[128]{0:T(128)S(1)}, s32[128]{0:T(128)}, u32[]{:S(2)}) copy-start(s32[128]{0:T(128)} %param.12) | copy-start | bytes 1540
  6.5 65.2 %all-gather.2.cloned.1.call-start = ((), (), s32[]{:S(2)}) async-start(), calls=%async_computation.1 | async-start | bytes 8912896 | tf_op jit(solution)/shard_map/all_gather | solution.py:12
  14.9 75.7 %all-to-all-start = ((s32[16,1,128]{2,1,0:T(1,128)}), s32[16,1,128]{2,1,0:T(1,128)S(1)}, u32[]{:S(2)}, u32[]{:S(2)}) async-start(s32[16,1,128]{2,1,0:T(1,128)} %stack.2), calls=%async_computation | async-start | bytes 16384 | tf_op jit(solution)/shard_map/all_to_all | solution.py:99
Sparse Core Ops, SparseCore 0:
  14.4 57.2 all-gather.1
